TPU v7x, 32 devices: a whole 2x2x4 slice. The times are simulated.
32 devices in a mesh: league: 2 (over x), seq: 16 (over z, y, core).
Axes of the slice: x: 2, y: 2, z: 4, core: 2. Of those that a mesh axis runs over, the one named last changes fastest.
Arguments:
- queries: bfloat16 [6144, 1792], P(('league', 'seq')), parts along dimension 0, may hold values from -100 to 100
- key_rows: bfloat16 [6144, 256], P(('league', 'seq')), parts along dimension 0, may hold values from -4 to 4
- value_rows: bfloat16 [6144, 256], P(('league', 'seq')), parts along dimension 0, may hold values from -6 to 6
- residual: bfloat16 [6144, 3584], P(('league', 'seq')), parts along dimension 0, may hold values from -6 to 6
- out_weight: bfloat16 [1792, 3584], P('seq'), may hold values from -0.125 to 0.125
- norm_gain: float32 [3584], replicated, may hold values from 0.1 to 1.9
- value_head: float32 [3584], replicated, may hold values from -0.09375 to 0.09375
- valid_length: int32 [2], P('league'), parts along dimension 0, may hold values from 1537 to 3072
Outputs:
- stream: bfloat16 [6144, 3584], P(('league', 'seq')), parts along dimension 0
- values: float32 [6144], P(('league', 'seq')), parts along dimension 0
There are 2 independent parts, one for each index of `league`. A program takes and returns all parts, laid end to end along the dimension named above; an argument that names none is the same for every part. Nothing has to cross between parts.
All inputs are finite; a program needn't handle non-finite values.
Results may differ from a plain program's by a relative error of at most 0.0085.
Values may be sent and summed in bfloat16 or wider, within the bound.
A program may use at most 128 MiB of HBM per device.

v0:
```python
import math
import jax
import jax.numpy as jnp
from jax import lax
from jax.sharding import PartitionSpec as P

HEAD_DIM = 128
NEG_BIG = -1e30


def row_positions(row_index, tok_count):
    owner_dev = row_index // tok_count
    within = row_index % tok_count
    return owner_dev * tok_count + within


def attend_block(
    carried, key_block, value_block, key_pos, query_grid, query_pos, query_limit, score_scale
):

    def run_block(carry_in):
        running_max, running_sum, running_out = carry_in
        scores = (
            jnp.einsum("qgrd,kgd->qgrk", query_grid, key_block, preferred_element_type=jnp.float32)
            * score_scale
        )
        allowed = key_pos[None, None, None, :] <= query_pos[:, None, None, None]
        new_max = jnp.maximum(running_max, jnp.max(jnp.where(allowed, scores, NEG_BIG), axis=-1))
        shrink = jnp.exp(running_max - new_max)
        weights = jnp.where(allowed, jnp.exp(scores - new_max[..., None]), 0.0)
        running_sum = running_sum * shrink + jnp.sum(weights, axis=-1)
        running_out = running_out * shrink[..., None] + jnp.einsum(
            "qgrk,kgd->qgrd",
            weights.astype(jnp.bfloat16),
            value_block,
            preferred_element_type=jnp.float32,
        )
        return (new_max, running_sum, running_out)

    def keep_block(carry_in):
        return carry_in

    needed = jnp.min(key_pos) <= query_limit
    return lax.cond(needed, run_block, keep_block, carried)


def attend_piece(
    carried, key_piece, value_piece, key_pos, query_grid, query_pos, query_limit, score_scale
):
    piece_rows = key_piece.shape[0]
    block_rows = math.gcd(piece_rows, 512)
    block_count = piece_rows // block_rows
    groups = key_piece.shape[1] // HEAD_DIM
    key_blocks = key_piece.reshape(block_count, block_rows, groups, HEAD_DIM)
    value_blocks = value_piece.reshape(block_count, block_rows, groups, HEAD_DIM)
    pos_blocks = key_pos.reshape(block_count, block_rows)

    def one_block(carry_in, inputs):
        return (
            attend_block(
                carry_in,
                inputs[0],
                inputs[1],
                inputs[2],
                query_grid,
                query_pos,
                query_limit,
                score_scale,
            ),
            None,
        )

    carried, unused = lax.scan(one_block, carried, (key_blocks, value_blocks, pos_blocks))
    return carried


def per_device(
    queries, key_rows, value_rows, residual, out_weight, norm_gain, value_head, valid_length
):
    device = lax.axis_index("seq")
    tok_count = queries.shape[0]
    valid_upto = valid_length[0]
    groups = key_rows.shape[1] // HEAD_DIM
    repeats = queries.shape[1] // key_rows.shape[1]
    score_scale = HEAD_DIM ** (-0.5)
    local_rows = jnp.arange(tok_count, dtype=jnp.int32)
    query_pos = row_positions(device * tok_count + local_rows, tok_count)
    query_ok = query_pos < valid_upto
    query_limit = jnp.max(jnp.where(query_ok, query_pos, -1))
    query_grid = queries.reshape(tok_count, groups, repeats, HEAD_DIM)
    start_state = (
        jnp.full((tok_count, groups, repeats), NEG_BIG, jnp.float32),
        jnp.zeros((tok_count, groups, repeats), jnp.float32),
        jnp.zeros((tok_count, groups, repeats, HEAD_DIM), jnp.float32),
    )
    key_piece = lax.all_gather(key_rows, "seq", axis=0, tiled=True)
    key_pos = row_positions(jnp.arange(key_piece.shape[0], dtype=jnp.int32), tok_count)
    carried = attend_piece(
        start_state,
        key_piece,
        lax.all_gather(value_rows, "seq", axis=0, tiled=True),
        key_pos,
        query_grid,
        query_pos,
        query_limit,
        score_scale,
    )
    running_max, running_sum, running_out = carried
    safe_sum = jnp.where(query_ok[:, None, None], running_sum, 1.0)
    attended = jnp.where(query_ok[:, None, None, None], running_out / safe_sum[..., None], 0.0)
    attended = attended.reshape(tok_count, groups * repeats * HEAD_DIM).astype(jnp.bfloat16)
    whole_weight = lax.all_gather(out_weight, "seq", axis=0, tiled=True)
    projected = jnp.dot(attended, whole_weight, preferred_element_type=jnp.float32)
    stream = (residual.astype(jnp.float32) + projected).astype(jnp.bfloat16)
    widened = stream.astype(jnp.float32)
    normed = widened * lax.rsqrt(jnp.mean(widened * widened, axis=-1, keepdims=True) + 1e-06)
    scored = jnp.sum(normed * (norm_gain * value_head)[None, :], axis=-1)
    natural_pos = device * tok_count + local_rows
    scored = jnp.where(natural_pos < valid_upto, scored, 0.0)
    return (stream, scored)


def solution(mesh):
    placed = (
        P(("league", "seq"), None),
        P(("league", "seq"), None),
        P(("league", "seq"), None),
        P(("league", "seq"), None),
        P("seq", None),
        P(),
        P(),
        P("league"),
    )
    return jax.shard_map(
        per_device,
        mesh=mesh,
        in_specs=placed,
        out_specs=(P(("league", "seq"), None), P(("league", "seq"))),
        check_vma=False,
    )
```

profile of v0, /device:TPU:0, one launch (start us, length us, event | category | flops | bytes accessed | tf_op | source)
XLA Modules:
  0.0 211.8 jit_solution(4323758560684722332)
XLA Ops:
  7.2 0.0 copy-start.1
  7.2 0.0 copy-start.2
  7.2 0.0 all-gather.4.cloned.1.call-start
  7.2 0.7 all-gather.4.cloned.1.call-update
  7.9 0.0 all-gather.6.cloned.1.call-start
  8.0 0.7 all-gather.6.cloned.1.call-update
  8.7 0.0 all-gather.8.cloned.1.call-start
  8.7 0.7 all-gather.8.cloned.1.call-update
  10.1 1.9 reshape.101
  12.0 0.2 copy.11
  12.2 0.0 copy-done.1
  12.2 0.0 copy-done.2
  12.2 0.6 select_reduce_fusion
  12.9 39.7 %all-gather.4.cloned.1.call-done = bf16[3072,256]{1,0:T(8,128)(2,1)} async-done(((bf16[192,256]{1,0:T(8,128)(2,1)}), bf16[3072,256]{1,0:T(8,128)(2,1)}) %all-gather.4.cloned.1.call-update) | async-done | bytes 1572880 | tf_op jit(solution)/shard_map/all_gather | solution.py:96
  52.6 2.4 %reshape.100 = bf16[6,512,2,128]{3,2,1,0:T(2,128)(2,1)S(1)} reshape(bf16[3072,256]{1,0:T(8,128)(2,1)} %all-gather.4.cloned.1.call-done) | data formatting | bytes 3145728 | tf_op jit(solution)/shard_map/reshape | solution.py:54
  55.0 1.4 copy.10
  56.4 36.8 %all-gather.6.cloned.1.call-done = bf16[3072,256]{1,0:T(8,128)(2,1)} async-done(((bf16[192,256]{1,0:T(8,128)(2,1)}), bf16[3072,256]{1,0:T(8,128)(2,1)}) %all-gather.6.cloned.1.call-update) | async-done | bytes 1572880 | tf_op jit(solution)/shard_map/all_gather | solution.py:101
  93.3 2.4 %reshape.102 = bf16[6,512,2,128]{3,2,1,0:T(2,128)(2,1)S(1)} reshape(bf16[3072,256]{1,0:T(8,128)(2,1)} %all-gather.6.cloned.1.call-done) | data formatting | bytes 3145728 | tf_op jit(solution)/shard_map/reshape | solution.py:55
  95.6 1.4 copy.12
  97.0 0.1 broadcast_in_dim.74
  97.2 19.7 %while.15 = (s32[]{:T(128)}, f32[192,2,7]{0,2,1:T(8,128)S(1)}, f32[192,2,7]{0,2,1:T(8,128)S(1)}, f32[192,2,7,128]{3,0,2,1:T(8,128)S(1)}, s32[6,512]{1,0:T(8,128)...) while((s32[]{:T(128)}, f32[192,2,7]{0,2,1:T(8,128)S(1)}, ...), condition=%wide.region_7.8_spmd.clone, body=%wide.region_1.7_spmd.clone.sunk | while | flops 720577664 | bytes 21064692 | solution.py:73
  97.2 0.7 fusion.52
  99.3 6.9 %conditional.3 = ((f32[192,2,7]{0,2,1:T(8,128)S(1)}, f32[192,2,7]{0,2,1:T(8,128)S(1)}, f32[192,2,7,128]{3,0,2,1:T(8,128)S(1)})) conditional(s32[]{:T(128)} %convert_element_type.48, (f32[192,2,7]{0,2,1:T(8,128)S(1)}, f32[192,2,7]{0,2,1:T(8,128)S(1)}, f32[192,2,7,128]{3,0,2,1:T(8,128)S(1)}) %tuple.53, (s32[1,512]{1,0:T(1,128)S(1)}, ...), branch_computations={%region_3.3_spmd, %region_4.6_spmd.clone} | conditional | flops 720575808 | bytes 21056228 | solution.py:44
  99.3 0.1 broadcast_compare_fusion
  99.5 2.0 fusion.2
  101.5 1.8 fusion.6
  103.3 2.9 %fusion.16 = f32[192,2,7,128]{3,0,2,1:T(8,128)S(1)} fusion(f32[2,512,192,7]{1,2,3,0:T(8,128)S(1)} %get-tuple-element.265, f32[192,2,7]{0,2,1:T(8,128)S(1)} %max.5, pred[192,512]{1,0:T(8,128)(4,1)S(1)} %broadcast_compare_fusion, f32[192,2,7,128]{3,0,2,1:T(8,128)S(1)} %get-tuple-element.208, f32[192,2,7]{0,2,1:T(8,128)S(1)} %get-tuple-element.261, ...), kind=kOutput, calls=%fused_computation.14 | convolution fusion | flops 358514688 | bytes 8640000 | tf_op jit(solution)/shard_map/while/body/eval_jaxpr/cond/branch_1_fun/qgrk,kgd->qgrd/dot_general | solution.py:32
  106.2 0.7 fusion.52
  108.3 0.7 fusion.52
  110.5 0.7 fusion.52
  112.6 0.7 fusion.52
  114.8 0.7 fusion.52
  116.9 0.5 select_convert_fusion
  117.4 0.5 copy.13
  117.9 0.7 convert_element_type.25
  118.6 77.7 %all-gather.8.cloned.1.call-done = bf16[1792,3584]{1,0:T(8,128)(2,1)} async-done(((bf16[112,3584]{1,0:T(8,128)(2,1)}), bf16[1792,3584]{1,0:T(8,128)(2,1)}) %all-gather.8.cloned.1.call-update) | async-done | bytes 12845072 | tf_op jit(solution)/shard_map/all_gather | solution.py:112
  196.3 7.8 %fusion.35 = (f32[192]{0:T(256)S(1)}, bf16[192,3584]{1,0:T(8,128)(2,1)S(1)}) fusion(bf16[192,1792]{1,0:T(8,128)(2,1)S(1)} %convert_element_type.25, bf16[1792,3584]{1,0:T(8,128)(2,1)} %all-gather.8.cloned.1.call-done, bf16[192,3584]{1,0:T(8,128)(2,1)} %param.15), kind=kOutput, calls=%fused_computation.42 | convolution fusion | flops 2470379264 | bytes 16286464 | tf_op jit(solution)/shard_map/dot_general | solution.py:113
  204.1 0.0 copy-start
  204.2 0.5 fusion.37
  204.7 0.6 compare_select_fusion
  205.3 0.0 copy-done
  (46 shorter events, 0.4 us)
Async XLA Ops:
  7.2 5.0 %copy-start.1 = (f32[3584]{0:T(1024)S(1)}, f32[3584]{0:T(1024)}, u32[]{:S(2)}) copy-start(f32[3584]{0:T(1024)} %param.17) | copy-start | bytes 43012
  7.2 5.0 %copy-start.2 = (f32[3584]{0:T(1024)S(1)}, f32[3584]{0:T(1024)}, u32[]{:S(2)}) copy-start(f32[3584]{0:T(1024)} %param.18) | copy-start | bytes 43012
  7.2 45.4 %all-gather.4.cloned.1.call-start = ((), (), s32[]{:S(2)}) async-start(), calls=%async_computation | async-start | bytes 1671168 | tf_op jit(solution)/shard_map/all_gather | solution.py:96
  7.9 85.3 %all-gather.6.cloned.1.call-start = ((), (), s32[]{:S(2)}) async-start(), calls=%async_computation.1 | async-start | bytes 1671168 | tf_op jit(solution)/shard_map/all_gather | solution.py:101
  8.7 187.7 %all-gather.8.cloned.1.call-start = ((), (), s32[]{:S(2)}) async-start(), calls=%async_computation.2 | async-start | bytes 13647872 | tf_op jit(solution)/shard_map/all_gather | solution.py:112
  204.1 1.1 copy-start
Sparse Core Ops, SparseCore 0:
  10.3 42.3 all-gather.3
  54.9 38.2 all-gather.5
  95.5 100.7 all-gather.7
where the time goes:
time: 212 us
  waiting for transfers between devices  156 us (74%)
  between operations  14.6 us (7%)
  matrix products  12.7 us (6%)
  local copies, waits for them, and re-layouts  11 us (5%)
  other arithmetic  8.68 us (4%)
  loops' own time  8.39 us (4%)
    all_gather x1, waiting for transfers between devices, per_device(): whole_weight = lax.all_gather(out_weight, 'seq', axis=0, tiled=True)  77.7 us
    all_gather x1, waiting for transfers between devices, per_device(): key_piece = lax.all_gather(key_rows, 'seq', axis=0, tiled=True)  39.7 us
    all_gather x1, waiting for transfers between devices, per_device(): lax.all_gather(value_rows, 'seq', axis=0, tiled=True)  36.8 us
    another operation x1, loops' own time, attend_piece(): lax.scan(one_block, carried, (key_blocks, value_blocks, pos_blocks))  8.26 us
    dot_general x1, matrix products, per_device(): jnp.dot(attended, whole_weight, preferred_element_type=jnp.float32)  7.8 us
    reduce_min x6, other arithmetic, attend_block(): needed = jnp.min(key_pos) <= query_limit  4.3 us
  transfers between devices with their start and end apart: 3, of which 3 were waited for; matrix products, arithmetic and copies ran while one was open for 11% of the time, Pallas kernels for 0%

commit v1 on v0

--- a/solution.py
+++ b/solution.py
@@ -109,7 +109,15 @@
     safe_sum = jnp.where(query_ok[:, None, None], running_sum, 1.0)
     attended = jnp.where(query_ok[:, None, None, None], running_out / safe_sum[..., None], 0.0)
     attended = attended.reshape(tok_count, groups * repeats * HEAD_DIM).astype(jnp.bfloat16)
-    whole_weight = lax.all_gather(out_weight, "seq", axis=0, tiled=True)
+    peers = lax.axis_size("seq")
+    block, blocks = (out_weight, [out_weight])
+    for _ in range(peers - 1):
+        block = lax.ppermute(block, "seq", [(i, (i + 1) % peers) for i in range(peers)])
+        blocks.insert(0, block)
+    row_of_blocks = jnp.concatenate(blocks, axis=0)
+    whole_weight = jnp.roll(
+        row_of_blocks, (lax.axis_index("seq") + 1) * out_weight.shape[0], axis=0
+    )
     projected = jnp.dot(attended, whole_weight, preferred_element_type=jnp.float32)
     stream = (residual.astype(jnp.float32) + projected).astype(jnp.bfloat16)
     widened = stream.astype(jnp.float32)

time: 212 us -> 366 us (1.73)
  the two profiles are of different devices: /device:TPU:0 before, /device:TPU:31 now
where the time goes in v1:
time: 366 us; the launch traced here: 364 us
  waiting for transfers between devices  133 us (36%)
  local copies, waits for them, and re-layouts  82.6 us (23%)
  starting transfers between devices  68.5 us (19%)
  matrix products  37.5 us (10%)
  other arithmetic  19.6 us (5%)
  between operations  14.9 us (4%)
  loops' own time  8.57 us (2%)
    ppermute x15, waiting for transfers between devices, per_device(): lax.ppermute(block, 'seq', [(i, (i + 1) % peers) for i in range(peers)])  133 us
    unnamed x74, local copies, waits for them, and re-layouts  70.9 us
    ppermute x15, starting transfers between devices, per_device(): lax.ppermute(block, 'seq', [(i, (i + 1) % peers) for i in range(peers)])  68.4 us
    dot_general x6, matrix products, run_block(): jnp.einsum('qgrk,kgd->qgrd', weights.astype(jnp.bfloat16), value_block, p...  16.8 us
    dot_general x6, matrix products, run_block(): jnp.einsum('qgrd,kgd->qgrk', query_grid, key_block, preferred_element_typ...  12.2 us
    reduce_sum x6, other arithmetic, run_block(): running_sum = running_sum * shrink + jnp.sum(weights, axis=-1)  10.6 us
    dot_general x1, matrix products, per_device(): jnp.dot(attended, whole_weight, preferred_element_type=jnp.float32)  8.51 us
    another operation x1, loops' own time, attend_piece(): lax.scan(one_block, carried, (key_blocks, value_blocks, pos_blocks))  8.21 us
  transfers between devices with their start and end apart: 17, of which 13 were waited for; matrix products, arithmetic and copies ran while one was open for 17% of the time, Pallas kernels for 0%

profile of v1, /device:TPU:31, one launch (start us, length us, event | category | flops | bytes accessed | tf_op | source)
XLA Modules:
  0.0 364.5 jit_solution(12840812587522723388)
XLA Ops:
  7.7 9.4 %collective-permute-done = bf16[112,3584]{1,0:T(8,128)(2,1)S(1)} collective-permute-done((bf16[112,3584]{1,0:T(8,128)(2,1)}, bf16[112,3584]{1,0:T(8,128)(2,1)S(1)}, u32[]{:S(2)}, u32[]{:S(2)}) %collective-permute-start) | collective-permute-done | bytes 802848 | tf_op jit(solution)/shard_map/ppermute | solution.py:115
  18.0 5.1 %collective-permute-start.1 = (bf16[112,3584]{1,0:T(8,128)(2,1)S(1)}, bf16[112,3584]{1,0:T(8,128)(2,1)S(1)}, u32[]{:S(2)}, u32[]{:S(2)}) collective-permute-start(bf16[112,3584]{1,0:T(8,128)(2,1)S(1)} %collective-permute-done), channel_id=1, source_target_pairs={{0,1},{1,2},{2,3},{3,4},{4,5},{5,6},{6,7},{7,8},{8,9},{9,10},{10,1... | collective-permute-start | bytes 2408456 | tf_op jit(solution)/shard_map/ppermute | solution.py:115
  23.1 9.1 %collective-permute-done.1 = bf16[112,3584]{1,0:T(8,128)(2,1)S(1)} collective-permute-done((bf16[112,3584]{1,0:T(8,128)(2,1)S(1)}, bf16[112,3584]{1,0:T(8,128)(2,1)S(1)}, u32[]{:S(2)}, u32[]{:S(2)}) %collective-permute-start.1) | collective-permute-done | bytes 802848 | tf_op jit(solution)/shard_map/ppermute | solution.py:115
  33.1 5.2 %collective-permute-start.2 = (bf16[112,3584]{1,0:T(8,128)(2,1)S(1)}, bf16[112,3584]{1,0:T(8,128)(2,1)S(1)}, u32[]{:S(2)}, u32[]{:S(2)}) collective-permute-start(bf16[112,3584]{1,0:T(8,128)(2,1)S(1)} %collective-permute-done.1), channel_id=1, source_target_pairs={{0,1},{1,2},{2,3},{3,4},{4,5},{5,6},{6,7},{7,8},{8,9},{9,10},{10,1... | collective-permute-start | bytes 2408456 | tf_op jit(solution)/shard_map/ppermute | solution.py:115
  38.3 9.1 %collective-permute-done.2 = bf16[112,3584]{1,0:T(8,128)(2,1)S(1)} collective-permute-done((bf16[112,3584]{1,0:T(8,128)(2,1)S(1)}, bf16[112,3584]{1,0:T(8,128)(2,1)S(1)}, u32[]{:S(2)}, u32[]{:S(2)}) %collective-permute-start.2) | collective-permute-done | bytes 802848 | tf_op jit(solution)/shard_map/ppermute | solution.py:115
  48.3 5.2 %collective-permute-start.3 = (bf16[112,3584]{1,0:T(8,128)(2,1)S(1)}, bf16[112,3584]{1,0:T(8,128)(2,1)S(1)}, u32[]{:S(2)}, u32[]{:S(2)}) collective-permute-start(bf16[112,3584]{1,0:T(8,128)(2,1)S(1)} %collective-permute-done.2), channel_id=1, source_target_pairs={{0,1},{1,2},{2,3},{3,4},{4,5},{5,6},{6,7},{7,8},{8,9},{9,10},{10,1... | collective-permute-start | bytes 2408456 | tf_op jit(solution)/shard_map/ppermute | solution.py:115
  53.5 9.1 %collective-permute-done.3 = bf16[112,3584]{1,0:T(8,128)(2,1)S(1)} collective-permute-done((bf16[112,3584]{1,0:T(8,128)(2,1)S(1)}, bf16[112,3584]{1,0:T(8,128)(2,1)S(1)}, u32[]{:S(2)}, u32[]{:S(2)}) %collective-permute-start.3) | collective-permute-done | bytes 802848 | tf_op jit(solution)/shard_map/ppermute | solution.py:115
  63.5 5.2 %collective-permute-start.4 = (bf16[112,3584]{1,0:T(8,128)(2,1)S(1)}, bf16[112,3584]{1,0:T(8,128)(2,1)S(1)}, u32[]{:S(2)}, u32[]{:S(2)}) collective-permute-start(bf16[112,3584]{1,0:T(8,128)(2,1)S(1)} %collective-permute-done.3), channel_id=1, source_target_pairs={{0,1},{1,2},{2,3},{3,4},{4,5},{5,6},{6,7},{7,8},{8,9},{9,10},{10,1... | collective-permute-start | bytes 2408456 | tf_op jit(solution)/shard_map/ppermute | solution.py:115
  68.7 9.1 %collective-permute-done.4 = bf16[112,3584]{1,0:T(8,128)(2,1)S(1)} collective-permute-done((bf16[112,3584]{1,0:T(8,128)(2,1)S(1)}, bf16[112,3584]{1,0:T(8,128)(2,1)S(1)}, u32[]{:S(2)}, u32[]{:S(2)}) %collective-permute-start.4) | collective-permute-done | bytes 802848 | tf_op jit(solution)/shard_map/ppermute | solution.py:115
  78.7 5.2 %collective-permute-start.5 = (bf16[112,3584]{1,0:T(8,128)(2,1)S(1)}, bf16[112,3584]{1,0:T(8,128)(2,1)S(1)}, u32[]{:S(2)}, u32[]{:S(2)}) collective-permute-start(bf16[112,3584]{1,0:T(8,128)(2,1)S(1)} %collective-permute-done.4), channel_id=1, source_target_pairs={{0,1},{1,2},{2,3},{3,4},{4,5},{5,6},{6,7},{7,8},{8,9},{9,10},{10,1... | collective-permute-start | bytes 2408456 | tf_op jit(solution)/shard_map/ppermute | solution.py:115
  83.9 9.1 %collective-permute-done.5 = bf16[112,3584]{1,0:T(8,128)(2,1)S(1)} collective-permute-done((bf16[112,3584]{1,0:T(8,128)(2,1)S(1)}, bf16[112,3584]{1,0:T(8,128)(2,1)S(1)}, u32[]{:S(2)}, u32[]{:S(2)}) %collective-permute-start.5) | collective-permute-done | bytes 802848 | tf_op jit(solution)/shard_map/ppermute | solution.py:115
  93.0 5.2 %collective-permute-start.6 = (bf16[112,3584]{1,0:T(8,128)(2,1)S(1)}, bf16[112,3584]{1,0:T(8,128)(2,1)S(1)}, u32[]{:S(2)}, u32[]{:S(2)}) collective-permute-start(bf16[112,3584]{1,0:T(8,128)(2,1)S(1)} %collective-permute-done.5), channel_id=1, source_target_pairs={{0,1},{1,2},{2,3},{3,4},{4,5},{5,6},{6,7},{7,8},{8,9},{9,10},{10,1... | collective-permute-start | bytes 2408456 | tf_op jit(solution)/shard_map/ppermute | solution.py:115
  98.3 9.0 %collective-permute-done.6 = bf16[112,3584]{1,0:T(8,128)(2,1)S(1)} collective-permute-done((bf16[112,3584]{1,0:T(8,128)(2,1)S(1)}, bf16[112,3584]{1,0:T(8,128)(2,1)S(1)}, u32[]{:S(2)}, u32[]{:S(2)}) %collective-permute-start.6) | collective-permute-done | bytes 802848 | tf_op jit(solution)/shard_map/ppermute | solution.py:115
  107.3 5.3 %collective-permute-start.7 = (bf16[112,3584]{1,0:T(8,128)(2,1)S(1)}, bf16[112,3584]{1,0:T(8,128)(2,1)S(1)}, u32[]{:S(2)}, u32[]{:S(2)}) collective-permute-start(bf16[112,3584]{1,0:T(8,128)(2,1)S(1)} %collective-permute-done.6), channel_id=1, source_target_pairs={{0,1},{1,2},{2,3},{3,4},{4,5},{5,6},{6,7},{7,8},{8,9},{9,10},{10,1... | collective-permute-start | bytes 2408456 | tf_op jit(solution)/shard_map/ppermute | solution.py:115
  112.6 9.8 %collective-permute-done.7 = bf16[112,3584]{1,0:T(8,128)(2,1)S(1)} collective-permute-done((bf16[112,3584]{1,0:T(8,128)(2,1)S(1)}, bf16[112,3584]{1,0:T(8,128)(2,1)S(1)}, u32[]{:S(2)}, u32[]{:S(2)}) %collective-permute-start.7) | collective-permute-done | bytes 802848 | tf_op jit(solution)/shard_map/ppermute | solution.py:115
  123.4 5.2 %collective-permute-start.8 = (bf16[112,3584]{1,0:T(8,128)(2,1)S(1)}, bf16[112,3584]{1,0:T(8,128)(2,1)S(1)}, u32[]{:S(2)}, u32[]{:S(2)}) collective-permute-start(bf16[112,3584]{1,0:T(8,128)(2,1)S(1)} %collective-permute-done.7), channel_id=1, source_target_pairs={{0,1},{1,2},{2,3},{3,4},{4,5},{5,6},{6,7},{7,8},{8,9},{9,10},{10,1... | collective-permute-start | bytes 2408456 | tf_op jit(solution)/shard_map/ppermute | solution.py:115
  128.5 15.4 %collective-permute-done.8 = bf16[112,3584]{1,0:T(8,128)(2,1)S(1)} collective-permute-done((bf16[112,3584]{1,0:T(8,128)(2,1)S(1)}, bf16[112,3584]{1,0:T(8,128)(2,1)S(1)}, u32[]{:S(2)}, u32[]{:S(2)}) %collective-permute-start.8) | collective-permute-done | bytes 802848 | tf_op jit(solution)/shard_map/ppermute | solution.py:115
  144.9 5.2 %collective-permute-start.9 = (bf16[112,3584]{1,0:T(8,128)(2,1)S(1)}, bf16[112,3584]{1,0:T(8,128)(2,1)S(1)}, u32[]{:S(2)}, u32[]{:S(2)}) collective-permute-start(bf16[112,3584]{1,0:T(8,128)(2,1)S(1)} %collective-permute-done.8), channel_id=1, source_target_pairs={{0,1},{1,2},{2,3},{3,4},{4,5},{5,6},{6,7},{7,8},{8,9},{9,10},{10,1... | collective-permute-start | bytes 2408456 | tf_op jit(solution)/shard_map/ppermute | solution.py:115
  150.1 9.1 %collective-permute-done.9 = bf16[112,3584]{1,0:T(8,128)(2,1)S(1)} collective-permute-done((bf16[112,3584]{1,0:T(8,128)(2,1)S(1)}, bf16[112,3584]{1,0:T(8,128)(2,1)S(1)}, u32[]{:S(2)}, u32[]{:S(2)}) %collective-permute-start.9) | collective-permute-done | bytes 802848 | tf_op jit(solution)/shard_map/ppermute | solution.py:115
  159.2 5.2 %collective-permute-start.10 = (bf16[112,3584]{1,0:T(8,128)(2,1)S(1)}, bf16[112,3584]{1,0:T(8,128)(2,1)S(1)}, u32[]{:S(2)}, u32[]{:S(2)}) collective-permute-start(bf16[112,3584]{1,0:T(8,128)(2,1)S(1)} %collective-permute-done.9), channel_id=1, source_target_pairs={{0,1},{1,2},{2,3},{3,4},{4,5},{5,6},{6,7},{7,8},{8,9},{9,10},{10,1... | collective-permute-start | bytes 2408456 | tf_op jit(solution)/shard_map/ppermute | solution.py:115
  164.4 9.1 %collective-permute-done.10 = bf16[112,3584]{1,0:T(8,128)(2,1)S(1)} collective-permute-done((bf16[112,3584]{1,0:T(8,128)(2,1)S(1)}, bf16[112,3584]{1,0:T(8,128)(2,1)S(1)}, u32[]{:S(2)}, u32[]{:S(2)}) %collective-permute-start.10) | collective-permute-done | bytes 802848 | tf_op jit(solution)/shard_map/ppermute | solution.py:115
  173.5 5.3 %collective-permute-start.11 = (bf16[112,3584]{1,0:T(8,128)(2,1)S(1)}, bf16[112,3584]{1,0:T(8,128)(2,1)S(1)}, u32[]{:S(2)}, u32[]{:S(2)}) collective-permute-start(bf16[112,3584]{1,0:T(8,128)(2,1)S(1)} %collective-permute-done.10), channel_id=1, source_target_pairs={{0,1},{1,2},{2,3},{3,4},{4,5},{5,6},{6,7},{7,8},{8,9},{9,10},{10,1... | collective-permute-start | bytes 2408456 | tf_op jit(solution)/shard_map/ppermute | solution.py:115
  178.8 9.8 %collective-permute-done.11 = bf16[112,3584]{1,0:T(8,128)(2,1)S(1)} collective-permute-done((bf16[112,3584]{1,0:T(8,128)(2,1)S(1)}, bf16[112,3584]{1,0:T(8,128)(2,1)S(1)}, u32[]{:S(2)}, u32[]{:S(2)}) %collective-permute-start.11) | collective-permute-done | bytes 802848 | tf_op jit(solution)/shard_map/ppermute | solution.py:115
  189.5 5.2 %collective-permute-start.12 = (bf16[112,3584]{1,0:T(8,128)(2,1)S(1)}, bf16[112,3584]{1,0:T(8,128)(2,1)}, u32[]{:S(2)}, u32[]{:S(2)}) collective-permute-start(bf16[112,3584]{1,0:T(8,128)(2,1)S(1)} %collective-permute-done.11), channel_id=1, source_target_pairs={{0,1},{1,2},{2,3},{3,4},{4,5},{5,6},{6,7},{7,8},{8,9},{9,10},{10,1... | collective-permute-start | bytes 2408456 | tf_op jit(solution)/shard_map/ppermute | solution.py:115
  194.6 15.4 %collective-permute-done.12 = bf16[112,3584]{1,0:T(8,128)(2,1)} collective-permute-done((bf16[112,3584]{1,0:T(8,128)(2,1)S(1)}, bf16[112,3584]{1,0:T(8,128)(2,1)}, u32[]{:S(2)}, u32[]{:S(2)}) %collective-permute-start.12) | collective-permute-done | bytes 802848 | tf_op jit(solution)/shard_map/ppermute | solution.py:115
  210.1 5.3 %collective-permute-start.13 = (bf16[112,3584]{1,0:T(8,128)(2,1)}, bf16[112,3584]{1,0:T(8,128)(2,1)}, u32[]{:S(2)}, u32[]{:S(2)}) collective-permute-start(bf16[112,3584]{1,0:T(8,128)(2,1)} %collective-permute-done.12), channel_id=1, source_target_pairs={{0,1},{1,2},{2,3},{3,4},{4,5},{5,6},{6,7},{7,8},{8,9},{9,10},{10,1... | collective-permute-start | bytes 2408456 | tf_op jit(solution)/shard_map/ppermute | solution.py:115
  216.0 2.6 reshape.101
  222.1 2.4 reshape.100
  225.9 2.4 reshape.102
  230.1 53.6 %while.15 = (s32[]{:T(128)}, f32[192,2,7]{0,2,1:T(8,128)S(1)}, f32[192,2,7]{0,2,1:T(8,128)S(1)}, f32[192,2,7,128]{3,0,2,1:T(8,128)S(1)}, s32[6,512]{1,0:T(8,128)...) while((s32[]{:T(128)}, f32[192,2,7]{0,2,1:T(8,128)S(1)}, ...), condition=%wide.region_7.8_spmd.clone, body=%wide.region_1.7_spmd.clone.sunk | while | flops 720577664 | bytes 21064692 | solution.py:73
  232.2 6.8 %conditional.3 = ((f32[192,2,7]{0,2,1:T(8,128)S(1)}, f32[192,2,7]{0,2,1:T(8,128)S(1)}, f32[192,2,7,128]{3,0,2,1:T(8,128)S(1)})) conditional(s32[]{:T(128)} %convert_element_type.48, (f32[192,2,7]{0,2,1:T(8,128)S(1)}, f32[192,2,7]{0,2,1:T(8,128)S(1)}, f32[192,2,7,128]{3,0,2,1:T(8,128)S(1)}) %tuple.53, (s32[1,512]{1,0:T(1,128)S(1)}, ...), branch_computations={%region_3.3_spmd, %region_4.6_spmd.clone} | conditional | flops 720575808 | bytes 21056228 | solution.py:44
  236.2 2.8 fusion.16
  241.1 6.8 %conditional.3 = ((f32[192,2,7]{0,2,1:T(8,128)S(1)}, f32[192,2,7]{0,2,1:T(8,128)S(1)}, f32[192,2,7,128]{3,0,2,1:T(8,128)S(1)})) conditional(s32[]{:T(128)} %convert_element_type.48, (f32[192,2,7]{0,2,1:T(8,128)S(1)}, f32[192,2,7]{0,2,1:T(8,128)S(1)}, f32[192,2,7,128]{3,0,2,1:T(8,128)S(1)}) %tuple.53, (s32[1,512]{1,0:T(1,128)S(1)}, ...), branch_computations={%region_3.3_spmd, %region_4.6_spmd.clone} | conditional | flops 720575808 | bytes 21056228 | solution.py:44
  245.1 2.8 fusion.16
  250.1 6.8 %conditional.3 = ((f32[192,2,7]{0,2,1:T(8,128)S(1)}, f32[192,2,7]{0,2,1:T(8,128)S(1)}, f32[192,2,7,128]{3,0,2,1:T(8,128)S(1)})) conditional(s32[]{:T(128)} %convert_element_type.48, (f32[192,2,7]{0,2,1:T(8,128)S(1)}, f32[192,2,7]{0,2,1:T(8,128)S(1)}, f32[192,2,7,128]{3,0,2,1:T(8,128)S(1)}) %tuple.53, (s32[1,512]{1,0:T(1,128)S(1)}, ...), branch_computations={%region_3.3_spmd, %region_4.6_spmd.clone} | conditional | flops 720575808 | bytes 21056228 | solution.py:44
  254.1 2.8 fusion.16
  259.0 6.8 %conditional.3 = ((f32[192,2,7]{0,2,1:T(8,128)S(1)}, f32[192,2,7]{0,2,1:T(8,128)S(1)}, f32[192,2,7,128]{3,0,2,1:T(8,128)S(1)})) conditional(s32[]{:T(128)} %convert_element_type.48, (f32[192,2,7]{0,2,1:T(8,128)S(1)}, f32[192,2,7]{0,2,1:T(8,128)S(1)}, f32[192,2,7,128]{3,0,2,1:T(8,128)S(1)}) %tuple.53, (s32[1,512]{1,0:T(1,128)S(1)}, ...), branch_computations={%region_3.3_spmd, %region_4.6_spmd.clone} | conditional | flops 720575808 | bytes 21056228 | solution.py:44
  263.0 2.8 fusion.16
  267.9 6.8 %conditional.3 = ((f32[192,2,7]{0,2,1:T(8,128)S(1)}, f32[192,2,7]{0,2,1:T(8,128)S(1)}, f32[192,2,7,128]{3,0,2,1:T(8,128)S(1)})) conditional(s32[]{:T(128)} %convert_element_type.48, (f32[192,2,7]{0,2,1:T(8,128)S(1)}, f32[192,2,7]{0,2,1:T(8,128)S(1)}, f32[192,2,7,128]{3,0,2,1:T(8,128)S(1)}) %tuple.53, (s32[1,512]{1,0:T(1,128)S(1)}, ...), branch_computations={%region_3.3_spmd, %region_4.6_spmd.clone} | conditional | flops 720575808 | bytes 21056228 | solution.py:44
  271.9 2.8 fusion.16
  276.9 6.8 %conditional.3 = ((f32[192,2,7]{0,2,1:T(8,128)S(1)}, f32[192,2,7]{0,2,1:T(8,128)S(1)}, f32[192,2,7,128]{3,0,2,1:T(8,128)S(1)})) conditional(s32[]{:T(128)} %convert_element_type.48, (f32[192,2,7]{0,2,1:T(8,128)S(1)}, f32[192,2,7]{0,2,1:T(8,128)S(1)}, f32[192,2,7,128]{3,0,2,1:T(8,128)S(1)}) %tuple.53, (s32[1,512]{1,0:T(1,128)S(1)}, ...), branch_computations={%region_3.3_spmd, %region_4.6_spmd.clone} | conditional | flops 720575808 | bytes 21056228 | solution.py:44
  280.8 2.8 fusion.16
  287.5 2.3 constant_dynamic-update-slice_fusion.31
  289.7 2.1 constant_dynamic-update-slice_fusion.30
  291.9 2.1 constant_dynamic-update-slice_fusion.29
  300.2 2.1 constant_dynamic-update-slice_fusion.25
  302.3 2.1 constant_dynamic-update-slice_fusion.24
  306.4 2.1 constant_dynamic-update-slice_fusion.22
  308.6 2.1 constant_dynamic-update-slice_fusion.21
  310.7 2.1 constant_dynamic-update-slice_fusion.20
  312.8 2.1 constant_dynamic-update-slice_fusion.19
  314.9 2.1 constant_dynamic-update-slice_fusion.18
  317.0 2.1 constant_dynamic-update-slice_fusion.17
  320.1 2.1 constant_dynamic-update-slice_fusion.15
  322.2 2.1 constant_dynamic-update-slice_fusion.14
  324.3 2.1 constant_dynamic-update-slice_fusion.13
  328.3 2.1 constant_dynamic-update-slice_fusion.10
  330.4 2.1 constant_dynamic-update-slice_fusion.9
  332.5 2.1 constant_dynamic-update-slice_fusion.8
  334.6 2.1 constant_dynamic-update-slice_fusion.7
  338.7 2.1 constant_dynamic-update-slice_fusion.5
  340.8 2.1 constant_dynamic-update-slice_fusion.4
  342.9 2.1 constant_dynamic-update-slice_fusion.3
  348.0 8.5 %fusion.42 = (f32[192]{0:T(256)S(1)}, bf16[192,3584]{1,0:T(8,128)(2,1)S(1)}) fusion(bf16[192,1792]{1,0:T(8,128)(2,1)S(1)} %convert_element_type.25, bf16[3584,3584]{1,0:T(8,128)(2,1)} %constant_dynamic-update-slice_fusion, s32[]{:T(128)S(6)} %select_n.88, bf16[192,3584]{1,0:T(8,128)(2,1)S(1)} %copy-done.19), kind=kOutput, calls=%fused_computation.44 | convolution fusion | flops 2470379264 | bytes 16286468 | tf_op jit(solution)/shard_map/dot_general | solution.py:121
  (156 shorter events, 63.8 us)
Async XLA Ops:
  7.2 214.9 %all-gather.3.cloned.1.call-start = ((), (), s32[]{:S(2)}) async-start(), calls=%async_computation | async-start | bytes 1671168 | tf_op jit(solution)/shard_map/all_gather | solution.py:96
  7.2 9.9 %collective-permute-start = (bf16[112,3584]{1,0:T(8,128)(2,1)}, bf16[112,3584]{1,0:T(8,128)(2,1)S(1)}, u32[]{:S(2)}, u32[]{:S(2)}) collective-permute-start(bf16[112,3584]{1,0:T(8,128)(2,1)} %param.16), channel_id=1, source_target_pairs={{0,1},{1,2},{2,3},{3,4},{4,5},{5,6},{6,7},{7,8},{8,9},{9,10},{10,1... | collective-permute-start | bytes 2408456 | tf_op jit(solution)/shard_map/ppermute | solution.py:115
  17.1 0.9 copy-start.1
  18.0 14.2 %collective-permute-start.1 = (bf16[112,3584]{1,0:T(8,128)(2,1)S(1)}, bf16[112,3584]{1,0:T(8,128)(2,1)S(1)}, u32[]{:S(2)}, u32[]{:S(2)}) collective-permute-start(bf16[112,3584]{1,0:T(8,128)(2,1)S(1)} %collective-permute-done), channel_id=1, source_target_pairs={{0,1},{1,2},{2,3},{3,4},{4,5},{5,6},{6,7},{7,8},{8,9},{9,10},{10,1... | collective-permute-start | bytes 2408456 | tf_op jit(solution)/shard_map/ppermute | solution.py:115
  32.2 0.9 copy-start.3
  33.1 14.3 %collective-permute-start.2 = (bf16[112,3584]{1,0:T(8,128)(2,1)S(1)}, bf16[112,3584]{1,0:T(8,128)(2,1)S(1)}, u32[]{:S(2)}, u32[]{:S(2)}) collective-permute-start(bf16[112,3584]{1,0:T(8,128)(2,1)S(1)} %collective-permute-done.1), channel_id=1, source_target_pairs={{0,1},{1,2},{2,3},{3,4},{4,5},{5,6},{6,7},{7,8},{8,9},{9,10},{10,1... | collective-permute-start | bytes 2408456 | tf_op jit(solution)/shard_map/ppermute | solution.py:115
  47.4 0.9 copy-start.5
  48.3 14.3 %collective-permute-start.3 = (bf16[112,3584]{1,0:T(8,128)(2,1)S(1)}, bf16[112,3584]{1,0:T(8,128)(2,1)S(1)}, u32[]{:S(2)}, u32[]{:S(2)}) collective-permute-start(bf16[112,3584]{1,0:T(8,128)(2,1)S(1)} %collective-permute-done.2), channel_id=1, source_target_pairs={{0,1},{1,2},{2,3},{3,4},{4,5},{5,6},{6,7},{7,8},{8,9},{9,10},{10,1... | collective-permute-start | bytes 2408456 | tf_op jit(solution)/shard_map/ppermute | solution.py:115
  62.6 0.9 copy-start.6
  63.5 14.3 %collective-permute-start.4 = (bf16[112,3584]{1,0:T(8,128)(2,1)S(1)}, bf16[112,3584]{1,0:T(8,128)(2,1)S(1)}, u32[]{:S(2)}, u32[]{:S(2)}) collective-permute-start(bf16[112,3584]{1,0:T(8,128)(2,1)S(1)} %collective-permute-done.3), channel_id=1, source_target_pairs={{0,1},{1,2},{2,3},{3,4},{4,5},{5,6},{6,7},{7,8},{8,9},{9,10},{10,1... | collective-permute-start | bytes 2408456 | tf_op jit(solution)/shard_map/ppermute | solution.py:115
  77.8 0.9 copy-start.7
  78.7 14.3 %collective-permute-start.5 = (bf16[112,3584]{1,0:T(8,128)(2,1)S(1)}, bf16[112,3584]{1,0:T(8,128)(2,1)S(1)}, u32[]{:S(2)}, u32[]{:S(2)}) collective-permute-start(bf16[112,3584]{1,0:T(8,128)(2,1)S(1)} %collective-permute-done.4), channel_id=1, source_target_pairs={{0,1},{1,2},{2,3},{3,4},{4,5},{5,6},{6,7},{7,8},{8,9},{9,10},{10,1... | collective-permute-start | bytes 2408456 | tf_op jit(solution)/shard_map/ppermute | solution.py:115
  93.0 123.0 %copy-start.8 = (bf16[112,3584]{1,0:T(8,128)(2,1)}, bf16[112,3584]{1,0:T(8,128)(2,1)S(1)}, u32[]{:S(2)}) copy-start(bf16[112,3584]{1,0:T(8,128)(2,1)S(1)} %collective-permute-done.5) | copy-start | bytes 2408452
  93.0 14.3 %collective-permute-start.6 = (bf16[112,3584]{1,0:T(8,128)(2,1)S(1)}, bf16[112,3584]{1,0:T(8,128)(2,1)S(1)}, u32[]{:S(2)}, u32[]{:S(2)}) collective-permute-start(bf16[112,3584]{1,0:T(8,128)(2,1)S(1)} %collective-permute-done.5), channel_id=1, source_target_pairs={{0,1},{1,2},{2,3},{3,4},{4,5},{5,6},{6,7},{7,8},{8,9},{9,10},{10,1... | collective-permute-start | bytes 2408456 | tf_op jit(solution)/shard_map/ppermute | solution.py:115
  98.2 127.7 %all-gather.5.cloned.1.call-start = ((), (), s32[]{:S(2)}) async-start(), calls=%async_computation.1 | async-start | bytes 1671168 | tf_op jit(solution)/shard_map/all_gather | solution.py:101
  107.3 114.7 %copy-start.9 = (bf16[112,3584]{1,0:T(8,128)(2,1)}, bf16[112,3584]{1,0:T(8,128)(2,1)S(1)}, u32[]{:S(2)}) copy-start(bf16[112,3584]{1,0:T(8,128)(2,1)S(1)} %collective-permute-done.6) | copy-start | bytes 2408452
  107.3 15.2 %collective-permute-start.7 = (bf16[112,3584]{1,0:T(8,128)(2,1)S(1)}, bf16[112,3584]{1,0:T(8,128)(2,1)S(1)}, u32[]{:S(2)}, u32[]{:S(2)}) collective-permute-start(bf16[112,3584]{1,0:T(8,128)(2,1)S(1)} %collective-permute-done.6), channel_id=1, source_target_pairs={{0,1},{1,2},{2,3},{3,4},{4,5},{5,6},{6,7},{7,8},{8,9},{9,10},{10,1... | collective-permute-start | bytes 2408456 | tf_op jit(solution)/shard_map/ppermute | solution.py:115
  122.5 0.9 copy-start.10
  123.4 20.6 %collective-permute-start.8 = (bf16[112,3584]{1,0:T(8,128)(2,1)S(1)}, bf16[112,3584]{1,0:T(8,128)(2,1)S(1)}, u32[]{:S(2)}, u32[]{:S(2)}) collective-permute-start(bf16[112,3584]{1,0:T(8,128)(2,1)S(1)} %collective-permute-done.7), channel_id=1, source_target_pairs={{0,1},{1,2},{2,3},{3,4},{4,5},{5,6},{6,7},{7,8},{8,9},{9,10},{10,1... | collective-permute-start | bytes 2408456 | tf_op jit(solution)/shard_map/ppermute | solution.py:115
  144.0 0.9 copy-start.11
  144.9 14.3 %collective-permute-start.9 = (bf16[112,3584]{1,0:T(8,128)(2,1)S(1)}, bf16[112,3584]{1,0:T(8,128)(2,1)S(1)}, u32[]{:S(2)}, u32[]{:S(2)}) collective-permute-start(bf16[112,3584]{1,0:T(8,128)(2,1)S(1)} %collective-permute-done.8), channel_id=1, source_target_pairs={{0,1},{1,2},{2,3},{3,4},{4,5},{5,6},{6,7},{7,8},{8,9},{9,10},{10,1... | collective-permute-start | bytes 2408456 | tf_op jit(solution)/shard_map/ppermute | solution.py:115
  159.2 62.9 %copy-start.12 = (bf16[112,3584]{1,0:T(8,128)(2,1)}, bf16[112,3584]{1,0:T(8,128)(2,1)S(1)}, u32[]{:S(2)}) copy-start(bf16[112,3584]{1,0:T(8,128)(2,1)S(1)} %collective-permute-done.9) | copy-start | bytes 2408452
  159.2 14.3 %collective-permute-start.10 = (bf16[112,3584]{1,0:T(8,128)(2,1)S(1)}, bf16[112,3584]{1,0:T(8,128)(2,1)S(1)}, u32[]{:S(2)}, u32[]{:S(2)}) collective-permute-start(bf16[112,3584]{1,0:T(8,128)(2,1)S(1)} %collective-permute-done.9), channel_id=1, source_target_pairs={{0,1},{1,2},{2,3},{3,4},{4,5},{5,6},{6,7},{7,8},{8,9},{9,10},{10,1... | collective-permute-start | bytes 2408456 | tf_op jit(solution)/shard_map/ppermute | solution.py:115
  173.5 56.6 %copy-start.13 = (bf16[112,3584]{1,0:T(8,128)(2,1)}, bf16[112,3584]{1,0:T(8,128)(2,1)S(1)}, u32[]{:S(2)}) copy-start(bf16[112,3584]{1,0:T(8,128)(2,1)S(1)} %collective-permute-done.10) | copy-start | bytes 2408452
  173.5 15.1 %collective-permute-start.11 = (bf16[112,3584]{1,0:T(8,128)(2,1)S(1)}, bf16[112,3584]{1,0:T(8,128)(2,1)S(1)}, u32[]{:S(2)}, u32[]{:S(2)}) collective-permute-start(bf16[112,3584]{1,0:T(8,128)(2,1)S(1)} %collective-permute-done.10), channel_id=1, source_target_pairs={{0,1},{1,2},{2,3},{3,4},{4,5},{5,6},{6,7},{7,8},{8,9},{9,10},{10,1... | collective-permute-start | bytes 2408456 | tf_op jit(solution)/shard_map/ppermute | solution.py:115
  188.6 0.9 copy-start.15
  189.5 20.6 %collective-permute-start.12 = (bf16[112,3584]{1,0:T(8,128)(2,1)S(1)}, bf16[112,3584]{1,0:T(8,128)(2,1)}, u32[]{:S(2)}, u32[]{:S(2)}) collective-permute-start(bf16[112,3584]{1,0:T(8,128)(2,1)S(1)} %collective-permute-done.11), channel_id=1, source_target_pairs={{0,1},{1,2},{2,3},{3,4},{4,5},{5,6},{6,7},{7,8},{8,9},{9,10},{10,1... | collective-permute-start | bytes 2408456 | tf_op jit(solution)/shard_map/ppermute | solution.py:115
  210.1 19.6 %collective-permute-start.13 = (bf16[112,3584]{1,0:T(8,128)(2,1)}, bf16[112,3584]{1,0:T(8,128)(2,1)}, u32[]{:S(2)}, u32[]{:S(2)}) collective-permute-start(bf16[112,3584]{1,0:T(8,128)(2,1)} %collective-permute-done.12), channel_id=1, source_target_pairs={{0,1},{1,2},{2,3},{3,4},{4,5},{5,6},{6,7},{7,8},{8,9},{9,10},{10,1... | collective-permute-start | bytes 2408456 | tf_op jit(solution)/shard_map/ppermute | solution.py:115
  229.7 57.8 %collective-permute-start.14 = (bf16[112,3584]{1,0:T(8,128)(2,1)}, bf16[112,3584]{1,0:T(8,128)(2,1)}, u32[]{:S(2)}, u32[]{:S(2)}) collective-permute-start(bf16[112,3584]{1,0:T(8,128)(2,1)} %collective-permute-done.13), channel_id=1, source_target_pairs={{0,1},{1,2},{2,3},{3,4},{4,5},{5,6},{6,7},{7,8},{8,9},{9,10},{10,1... | collective-permute-start | bytes 2408456 | tf_op jit(solution)/shard_map/ppermute | solution.py:115
  283.7 35.4 %copy-start = (bf16[112,3584]{1,0:T(8,128)(2,1)S(1)}, bf16[112,3584]{1,0:T(8,128)(2,1)}, u32[]{:S(2)}) copy-start(bf16[112,3584]{1,0:T(8,128)(2,1)} %param.16) | copy-start | bytes 2408452
  284.2 60.9 %copy-start.4 = (bf16[112,3584]{1,0:T(8,128)(2,1)S(1)}, bf16[112,3584]{1,0:T(8,128)(2,1)}, u32[]{:S(2)}) copy-start(bf16[112,3584]{1,0:T(8,128)(2,1)} %copy-done.3) | copy-start | bytes 2408452
  284.2 61.8 %copy-start.2 = (bf16[112,3584]{1,0:T(8,128)(2,1)S(1)}, bf16[112,3584]{1,0:T(8,128)(2,1)}, u32[]{:S(2)}) copy-start(bf16[112,3584]{1,0:T(8,128)(2,1)} %copy-done.1) | copy-start | bytes 2408452
  287.4 38.9 %copy-start.16 = (bf16[112,3584]{1,0:T(8,128)(2,1)S(1)}, bf16[112,3584]{1,0:T(8,128)(2,1)}, u32[]{:S(2)}) copy-start(bf16[112,3584]{1,0:T(8,128)(2,1)} %copy-done.15) | copy-start | bytes 2408452
  287.4 39.9 %copy-start.14 = (bf16[112,3584]{1,0:T(8,128)(2,1)S(1)}, bf16[112,3584]{1,0:T(8,128)(2,1)}, u32[]{:S(2)}) copy-start(bf16[112,3584]{1,0:T(8,128)(2,1)} %copy-done.13) | copy-start | bytes 2408452
  287.5 60.5 %copy-start.19 = (bf16[192,3584]{1,0:T(8,128)(2,1)S(1)}, bf16[192,3584]{1,0:T(8,128)(2,1)}, u32[]{:S(2)}) copy-start(bf16[192,3584]{1,0:T(8,128)(2,1)} %param.15) | copy-start | bytes 4128772
  327.3 29.2 %copy-start.18 = (f32[3584]{0:T(1024)S(1)}, f32[3584]{0:T(1024)}, u32[]{:S(2)}) copy-start(f32[3584]{0:T(1024)} %mul.78) | copy-start | bytes 43012
  356.5 1.1 copy-start.17
Sparse Core Ops, SparseCore 0:
  98.3 46.9 all-gather.2
  164.5 46.7 all-gather.4
